TPU v7x, 32 devices: a whole 2x2x4 slice. The times are simulated.
32 devices in a mesh: dp: 4 (over x, y), tp: 8 (over z, core).
Axes of the slice: x: 2, y: 2, z: 4, core: 2. Of those that a mesh axis runs over, the one named last changes fastest.
Arguments:
- x: bfloat16 [7168, 5120], P(('dp', 'tp')), parts along dimension 0
- w_gate: bfloat16 [5120, 12288], P(None, 'tp')
- w_up: bfloat16 [5120, 12288], P(None, 'tp')
- w_down: bfloat16 [12288, 5120], P('tp')
Outputs:
- output: bfloat16 [7168, 5120], P(('dp', 'tp')), parts along dimension 0
There are 4 independent parts. A program takes and returns all parts, laid end to end along the dimension named above; an argument that names none is the same for every part.
All inputs are finite; a program needn't handle non-finite values.
Results may differ from a plain program's by a relative error of at most 0.016.
Values are sent between devices in bfloat16 or wider.
A program may use at most 2 GiB of HBM per device.

v0:
```python
import jax
import jax.numpy as jnp
from jax import lax
from jax.sharding import PartitionSpec as P


def solution(mesh):
    def step(x, w_gate, w_up, w_down):
        rows = lax.all_gather(x, "tp", axis=0, tiled=True)
        gate = jnp.dot(rows, w_gate, preferred_element_type=jnp.float32)
        up = jnp.dot(rows, w_up, preferred_element_type=jnp.float32)
        hidden = (jax.nn.silu(gate) * up).astype(jnp.bfloat16)
        term = jnp.dot(hidden, w_down, preferred_element_type=jnp.float32).astype(jnp.bfloat16)
        return lax.psum_scatter(term, "tp", scatter_dimension=0, tiled=True)

    return jax.shard_map(
        step,
        mesh=mesh,
        in_specs=(P(("dp", "tp"), None), P(None, "tp"), P(None, "tp"), P("tp", None)),
        out_specs=P(("dp", "tp"), None),
        check_vma=False,
    )
```

profile of v0, /device:TPU:0, one launch (start us, length us, event | category | flops | bytes accessed | tf_op | source)
XLA Modules:
  0.0 473.8 jit_solution(12845725144496409934)
XLA Ops:
  6.5 0.0 all-gather.2.cloned.1.call-start
  6.5 0.7 all-gather.2.cloned.1.call-update
  7.3 0.0 reduce-scatter.2.cloned.1.call-start
  7.3 168.4 %all-gather.2.cloned.1.call-done = bf16[1792,5120]{1,0:T(8,128)(2,1)} async-done(((bf16[224,5120]{1,0:T(8,128)(2,1)}), bf16[1792,5120]{1,0:T(8,128)(2,1)}) %all-gather.2.cloned.1.call-update) | async-done | bytes 18350096 | tf_op jit(solution)/shard_map/all_gather | solution.py:9
  175.8 0.0 slice-start
  175.8 0.0 slice-start.1
  175.8 37.6 %fusion = f32[1792,1536]{1,0:T(8,128)} fusion(bf16[1792,5120]{1,0:T(8,128)(2,1)} %all-gather.2.cloned.1.call-done, bf16[5120,1536]{1,0:T(8,128)(2,1)} %param.5), kind=kOutput, calls=%fused_computation.2 | convolution fusion | flops 28185722880 | bytes 45088768 | tf_op jit(solution)/shard_map/dot_general | solution.py:10
  213.3 0.0 slice-start.2
  213.3 0.0 slice-start.3
  213.3 38.3 %multiply_convert_fusion = bf16[1792,1536]{1,0:T(8,128)(2,1)} fusion(f32[1792,1536]{1,0:T(8,128)} %fusion, bf16[1792,5120]{1,0:T(8,128)(2,1)} %all-gather.2.cloned.1.call-done, bf16[5120,1536]{1,0:T(8,128)(2,1)} %param.6), kind=kOutput, calls=%fused_computation.1 | convolution fusion | flops 28202237952 | bytes 50593792 | tf_op jit(solution)/shard_map/dot_general | solution.py:11
  251.6 0.0 slice-done
  251.6 0.0 slice-done.1
  251.6 0.0 slice-done.2
  251.6 0.0 slice-done.3
  251.6 33.6 %convolution_convert_fusion = bf16[1792,5120]{1,0:T(8,128)(2,1)} fusion(bf16[1792,1536]{1,0:T(8,128)(2,1)} %multiply_convert_fusion, bf16[1536,5120]{1,0:T(8,128)(2,1)S(1)} %bitcast.7), kind=kOutput, calls=%fused_computation | convolution fusion | flops 28194897920 | bytes 39583744 | tf_op jit(solution)/shard_map/dot_general | solution.py:13
  285.2 0.0 reduce-scatter.2.cloned.1.call-update
  285.3 181.7 %reduce-scatter.2.cloned.1.call-done = bf16[224,5120]{1,0:T(8,128)(2,1)} async-done(((bf16[1792,5120]{1,0:T(8,128)(2,1)}), bf16[224,5120]{1,0:T(8,128)(2,1)}) %reduce-scatter.2.cloned.1.call-update) | async-done | bytes 2293776 | tf_op jit(solution)/shard_map/reduce_scatter | solution.py:14
  (1 shorter events, 0.0 us)
Async XLA Ops:
  6.5 169.2 %all-gather.2.cloned.1.call-start = ((), (), s32[]{:S(2)}) async-start(), calls=%async_computation.1 | async-start | bytes 20643840 | tf_op jit(solution)/shard_map/all_gather | solution.py:9
  7.3 459.7 %reduce-scatter.2.cloned.1.call-start = ((), (), s32[]{:S(2)}) async-start(), calls=%async_computation.2 | async-start | bytes 20643840 | tf_op jit(solution)/shard_map/reduce_scatter | solution.py:14
  175.8 75.9 %slice-start = ((s8[15728640]{0:T(1024)(128)(4,1)}), s8[4194304]{0:T(1024)(128)(4,1)S(1)}, s32[]{:S(2)}) async-start(s8[15728640]{0:T(1024)(128)(4,1)} %bitcast.6), calls=%async_computation.3 | async-start | bytes 8388608
  175.8 75.9 %slice-start.1 = ((s8[15728640]{0:T(1024)(128)(4,1)}), s8[4194304]{0:T(1024)(128)(4,1)S(1)}, s32[]{:S(2)}) async-start(s8[15728640]{0:T(1024)(128)(4,1)} %bitcast.6), calls=%async_computation.4 | async-start | bytes 8388608
  213.3 38.3 %slice-start.2 = ((s8[15728640]{0:T(1024)(128)(4,1)}), s8[4194304]{0:T(1024)(128)(4,1)S(1)}, s32[]{:S(2)}) async-start(s8[15728640]{0:T(1024)(128)(4,1)} %bitcast.6), calls=%async_computation.5 | async-start | bytes 8388608
  213.3 38.3 %slice-start.3 = ((s8[15728640]{0:T(1024)(128)(4,1)}), s8[3145728]{0:T(1024)(128)(4,1)S(1)}, s32[]{:S(2)}) async-start(s8[15728640]{0:T(1024)(128)(4,1)} %bitcast.6), calls=%async_computation.6 | async-start | bytes 6291456
Sparse Core Ops, SparseCore 0:
  9.0 166.7 all-gather.1
  285.4 181.5 reduce-scatter.1
where the time goes:
time: 474 us
  waiting for transfers between devices  351 us (74%)
  matrix products  109 us (23%)
  between operations  13.4 us (3%)
    reduce_scatter x1, waiting for transfers between devices, step(): return lax.psum_scatter(term, 'tp', scatter_dimension=0, tiled=True)  182 us
    all_gather x1, waiting for transfers between devices, step(): rows = lax.all_gather(x, 'tp', axis=0, tiled=True)  168 us
    dot_general x1, matrix products, step(): up = jnp.dot(rows, w_up, preferred_element_type=jnp.float32)  38.3 us
    dot_general x1, matrix products, step(): gate = jnp.dot(rows, w_gate, preferred_element_type=jnp.float32)  37.6 us
    dot_general x1, matrix products, step(): jnp.dot(hidden, w_down, preferred_element_type=jnp.float32)  33.6 us
  transfers between devices with their start and end apart: 2, of which 2 were waited for; matrix products, arithmetic and copies ran while one was open for 0% of the time, Pallas kernels for 0%

commit v1 on v0

v1 whole, which is shorter than its diff:
```python
import jax
import jax.numpy as jnp
from jax import lax
from jax.experimental import pallas as pl
from jax.experimental.pallas import tpu as pltpu
from jax.sharding import PartitionSpec as P

MESH = pl.DeviceIdType.MESH
CHIPS = 4
SUBS = 2
CHUNKS = 10
LAG = 3
RING = 4
TILES = 3


def kernel(
    x, wg, wu, wd, y, xg,
    wgv, wuv, wdv, xb, hid, rin, own0, snd, term, give, take,
    ag_s, ag_r, dd_s, dd_r, os, orr, rin_r, own_r, snd_s, give_s, take_r, y_s, w_s, x_s, credit,
):
    f32, bf16 = jnp.float32, jnp.bfloat16
    half, depth = x.shape[0] // 2, x.shape[1]
    piece, width, tile = half // SUBS, depth // CHUNKS, wg.shape[1] // TILES
    t = lax.axis_index("tp")
    z, c = t // 2, t % 2
    other = t + 1 - 2 * c
    pos = (z, CHIPS - 1 - z)
    ahead, behind = (t + 2, t - 2), (t - 2, t + 2)
    inner = jnp.minimum(z, CHIPS - 1 - z)
    low = z < 2

    def remote(src, dst, send, recv, device):
        return pltpu.make_async_remote_copy(
            src_ref=src, dst_ref=dst, send_sem=send, recv_sem=recv, device_id={"tp": device}, device_id_type=MESH
        )

    def slab(j, h, core):
        return (j * 2 + h) * 2 + core

    def rows(i):
        return pl.ds(i * piece, piece)

    def cols(i, n):
        return pl.ds(pl.multiple_of(i * n, n), n)

    barrier = pltpu.get_barrier_semaphore()
    pl.semaphore_signal(barrier, inc=1, device_id={"tp": other}, device_id_type=MESH)
    for d in range(2):
        @pl.when(pos[d] < CHIPS - 1)
        def _():
            pl.semaphore_signal(barrier, inc=1, device_id={"tp": ahead[d]}, device_id_type=MESH)
    pl.semaphore_wait(barrier, 1 + jnp.minimum(z, 1) + jnp.minimum(CHIPS - 1 - z, 1))

    def send_own(d, h, slot, i):
        return remote(
            x.at[pl.ds(h * half + i * piece, piece)], xg.at[slab(z, h, c), rows(i)],
            ag_s.at[d, slot, i], ag_r.at[d, slot, i], ahead[d],
        )

    def give_own(h):
        return remote(x.at[pl.ds(h * half, half)], xg.at[slab(z, h, c)], os.at[h], orr.at[h], other)

    for d in range(2):
        @pl.when(pos[d] < CHIPS - 1)
        def _():
            for i in range(SUBS):
                send_own(d, 0, 0, i).start()
    give_own(0).start()

    def weight(k, src, dst, i):
        return pltpu.make_async_copy(src.at[:, cols(i, tile)], dst.at[:, cols(i, tile)], w_s.at[k, i])

    for i in range(TILES):
        weight(0, wg, wgv, i).start()
        weight(1, wu, wuv, i).start()
    load_wd = pltpu.make_async_copy(wd, wdv, w_s.at[2, 0])
    load_wd.start()
    give_own(1).start()

    def hidden_slot(a):
        return jnp.where(a == 0, 0, 1 + (a - 1) % 3)

    def forward(s):
        far = CHIPS - 1 - inner
        j = jnp.where(s <= far, inner + s, inner + 2 * far + 1 - s)
        h = jnp.where(s <= far, 0, 1)
        near = s > 2 * far
        j = jnp.where(near, 0, j)
        h = jnp.where(near, s - 5, h)
        slot = jnp.where(near, s - 5, s - 1)
        j = jnp.where(low, j, CHIPS - 1 - j)
        came = jnp.where(low, 1, 0)
        came = jnp.where(near, 1 - came, came)
        mine = pltpu.make_async_copy(x.at[pl.ds(0, half)], xb.at[pl.ds(0, half)], x_s.at[0])
        theirs = pltpu.make_async_copy(xg.at[0], xb.at[pl.ds(half, half)], x_s.at[1])

        @pl.when((s == 0) | (s == 7))
        def _():
            ho = s // 7
            pltpu.make_async_copy(
                x.at[pl.ds(pl.multiple_of(ho * half, half), half)], xb.at[pl.ds(0, half)], x_s.at[0]
            ).start()
            give_own(ho).wait_recv()
            pltpu.make_async_copy(xg.at[slab(z, ho, 1 - c)], xb.at[pl.ds(half, half)], x_s.at[1]).start()

        @pl.when((s > 0) & (s < 7))
        def _():
            pltpu.make_async_copy(xg.at[slab(j, h, c)], xb.at[pl.ds(0, half)], x_s.at[0]).start()
            for i in range(SUBS):
                spot = xg.at[slab(j, h, 1 - c), rows(i)]
                remote(spot, spot, dd_s.at[came, slot, i], dd_r.at[came, slot, i], other).wait_recv()
            pltpu.make_async_copy(xg.at[slab(j, h, 1 - c)], xb.at[pl.ds(half, half)], x_s.at[1]).start()

        mine.wait()
        theirs.wait()
        hs = hidden_slot(s)

        @pl.loop(0, TILES)
        def _(i):
            @pl.when(s == 0)
            def _():
                weight(0, wg, wgv, i).wait()
                weight(1, wu, wuv, i).wait()

            gate = jnp.dot(xb[...], wgv[:, cols(i, tile)], preferred_element_type=f32)
            up = jnp.dot(xb[...], wuv[:, cols(i, tile)], preferred_element_type=f32)
            hid[hs, :, cols(i, tile)] = (jax.nn.silu(gate) * up).astype(bf16)

    def relay(s, i):
        for d in range(2):
            @pl.when((pos[d] > 0) & (s < 2 * pos[d]))
            def _():
                p = pos[d] - 1
                j = jnp.where(s <= p, p - s, s - p - 1)
                h = jnp.where(s <= p, 0, 1)
                spot = xg.at[slab(j if d == 0 else CHIPS - 1 - j, h, c), rows(i)]
                remote(spot, spot, ag_s.at[d, s, i], ag_r.at[d, s, i], ahead[d]).wait_recv()

                @pl.when(pos[d] < CHIPS - 1)
                def _():
                    remote(spot, spot, ag_s.at[d, s + 1, i], ag_r.at[d, s + 1, i], ahead[d]).start()

                remote(spot, spot, dd_s.at[d, s, i], dd_r.at[d, s, i], other).start()

    def exchange(b, i):
        return remote(give.at[b, i % RING], take.at[b, i], give_s.at[b, i % RING], take_r.at[b, i], other)

    def make_term(b, hs, i):
        value = jnp.dot(hid[hs], wdv[:, cols(i, width)], preferred_element_type=f32)
        term[b, i % RING] = value[:half]

        @pl.when(i >= RING)
        def _():
            exchange(b, i - RING).wait_send()

        give[b, i % RING] = value[half:].astype(bf16)
        exchange(b, i).start()

    def drain(b):
        for i in range(CHUNKS - RING, CHUNKS):
            exchange(b, i).wait_send()

    def to_ring(d, i):
        return remote(snd.at[d, i], rin.at[d, i], snd_s.at[d, i], rin_r.at[d, i], ahead[d])

    def to_own(d, i):
        return remote(snd.at[d, i], own0.at[d, i], snd_s.at[d, i], own_r.at[d, i], ahead[d])

    def scatter(s):
        active = [(pos[d] < CHIPS - 1) & (s >= 2 * pos[d] + 1) & (s < 7) for d in range(2)]

        @pl.when(active[0] | active[1])
        def _():
            @pl.loop(0, CHUNKS + LAG)
            def _(i):
                for d in range(2):
                    far = low if d == 0 else jnp.logical_not(low)

                    @pl.when(active[d] & (i < CHUNKS))
                    def _():
                        make_term(d, hidden_slot(s - jnp.where(far, 2 * inner, 0)), i)

                for d in range(2):
                    @pl.when(active[d] & (i >= LAG))
                    def _():
                        k = i - LAG
                        r = s - 2 * pos[d] - 1
                        exchange(d, k).wait_recv()

                        @pl.when(pos[d] > 0)
                        def _():
                            to_ring(d, k).wait_recv()
                            term[d, k % RING] = term[d, k % RING] + rin[d, k].astype(f32)
                            pl.semaphore_signal(credit.at[d], inc=1, device_id={"tp": behind[d]}, device_id_type=MESH)

                        @pl.when(r >= 1)
                        def _():
                            to_ring(d, k).wait_send()

                        snd[d, k] = (term[d, k % RING] + take[d, k].astype(f32)).astype(bf16)

                        @pl.when(r == 0)
                        def _():
                            to_own(d, k).start()

                        @pl.when(r >= 2)
                        def _():
                            pl.semaphore_wait(credit.at[d], 1)

                        @pl.when(r >= 1)
                        def _():
                            to_ring(d, k).start()

            for d in range(2):
                @pl.when(active[d])
                def _():
                    drain(d)

    def write(h, i):
        spot = (pl.ds(h * half, half), cols(i, width))
        return pltpu.make_async_copy(xb.at[spot], y.at[spot], y_s.at[h, i])

    def finish(h, hs):
        came, sems = (own0, own_r) if h == 0 else (rin, rin_r)

        @pl.loop(0, CHUNKS + LAG)
        def _(i):
            @pl.when(i < CHUNKS)
            def _():
                make_term(h, hs, i)

            @pl.when(i >= LAG)
            def _():
                k = i - LAG
                exchange(h, k).wait_recv()
                term[h, k % RING] = term[h, k % RING] + take[h, k].astype(f32)
                for d in range(2):
                    @pl.when(pos[d] > 0)
                    def _():
                        remote(came.at[d, k], came.at[d, k], snd_s.at[d, k], sems.at[d, k], ahead[d]).wait_recv()
                        term[h, k % RING] = term[h, k % RING] + came[d, k].astype(f32)

                xb[pl.ds(h * half, half), cols(k, width)] = term[h, k % RING].astype(bf16)
                write(h, k).start()

        drain(h)

    @pl.loop(0, 8)
    def _(s):
        for d in range(2):
            @pl.when((pos[d] < CHIPS - 1) & (s == 2 * pos[d]))
            def _():
                for i in range(SUBS):
                    send_own(d, 1, s + 1, i).start()

        forward(s)

        @pl.when(s == 0)
        def _():
            load_wd.wait()

        relay(s, 0)
        scatter(s)
        for i in range(1, SUBS):
            relay(s, i)

    finish(0, 0)
    finish(1, 1)

    for h in range(2):
        give_own(h).wait_send()

        @pl.loop(0, CHUNKS)
        def _(i):
            write(h, i).wait()

    for d in range(2):
        for s in range(6):
            for i in range(SUBS):
                spot = xg.at[0, rows(i)]

                @pl.when((pos[d] < CHIPS - 1) & (s < 2 * pos[d] + 2))
                def _():
                    remote(spot, spot, ag_s.at[d, s, i], ag_r.at[d, s, i], ahead[d]).wait_send()

                @pl.when(s < 2 * pos[d])
                def _():
                    remote(spot, spot, dd_s.at[d, s, i], dd_r.at[d, s, i], other).wait_send()

        @pl.when(pos[d] < CHIPS - 1)
        def _():
            @pl.loop(0, CHUNKS)
            def _(i):
                to_ring(d, i).wait_send()


def block(x, w_gate, w_up, w_down):
    (n, depth), hidden = x.shape, w_gate.shape[1]
    half, width = n // 2, depth // CHUNKS
    f32, bf16, sem = jnp.float32, jnp.bfloat16, pltpu.SemaphoreType
    return pl.pallas_call(
        kernel,
        name="mlp_line",
        out_shape=(
            jax.ShapeDtypeStruct((n, depth), bf16),
            jax.ShapeDtypeStruct((4 * CHIPS, half, depth), bf16),
        ),
        in_specs=[pl.BlockSpec(memory_space=pl.ANY)] * 4,
        out_specs=(pl.BlockSpec(memory_space=pl.ANY),) * 2,
        scratch_shapes=[
            pltpu.VMEM((depth, hidden), bf16),
            pltpu.VMEM((depth, hidden), bf16),
            pltpu.VMEM((hidden, depth), bf16),
            pltpu.VMEM((n, depth), bf16),
            pltpu.VMEM((4, n, hidden), bf16),
            pltpu.VMEM((2, CHUNKS, half, width), bf16),
            pltpu.VMEM((2, CHUNKS, half, width), bf16),
            pltpu.VMEM((2, CHUNKS, half, width), bf16),
            pltpu.VMEM((2, RING, half, width), f32),
            pltpu.VMEM((2, RING, half, width), bf16),
            pltpu.VMEM((2, CHUNKS, half, width), bf16),
            sem.DMA((2, 6, SUBS)),
            sem.DMA((2, 6, SUBS)),
            sem.DMA((2, 6, SUBS)),
            sem.DMA((2, 6, SUBS)),
            sem.DMA((2,)),
            sem.DMA((2,)),
            sem.DMA((2, CHUNKS)),
            sem.DMA((2, CHUNKS)),
            sem.DMA((2, CHUNKS)),
            sem.DMA((2, RING)),
            sem.DMA((2, CHUNKS)),
            sem.DMA((2, CHUNKS)),
            sem.DMA((3, TILES)),
            sem.DMA((2,)),
            sem.REGULAR((2,)),
        ],
        compiler_params=pltpu.CompilerParams(
            collective_id=0, has_side_effects=True, vmem_limit_bytes=67_043_328
        ),
    )(x, w_gate, w_up, w_down)[0]


def solution(mesh):
    return jax.shard_map(
        block,
        mesh=mesh,
        in_specs=(P(("dp", "tp"), None), P(None, "tp"), P(None, "tp"), P("tp", None)),
        out_specs=P(("dp", "tp"), None),
        check_vma=False,
    )
```

time: 474 us -> 238 us (0.50)
  waiting for transfers between devices: 351 us -> 0 us
  Pallas kernels: 0 us -> 235 us
  matrix products: 109 us -> 0 us
  between operations: 13.4 us -> 0.01 us
    pallas_call x0 -> x1, Pallas kernels: none -> 235 us  [block(): pl.pallas_call(kernel, name='mlp_line', out_shape=(jax.ShapeDtypeStruct((...]
    reduce_scatter x1 -> x0, waiting for transfers between devices: 182 us -> none  [step(): return lax.psum_scatter(term, 'tp', scatter_dimension=0, tiled=True)]
    all_gather x1 -> x0, waiting for transfers between devices: 168 us -> none  [step(): rows = lax.all_gather(x, 'tp', axis=0, tiled=True)]
    dot_general x3 -> x0, matrix products: 109 us -> none  [the longest x1 38.3 us: step(): up = jnp.dot(rows, w_up, preferred_element_type=jnp.float32)]
  transfers between devices with their start and end apart: 2 -> 0, of which waited for: 2 -> 0; matrix products, arithmetic and copies ran while one was open for 0% -> 0% of each run, Pallas kernels for 0% -> 0%
where the time goes in v1:
time: 238 us
  Pallas kernels  235 us (99%)
  local copies, waits for them, and re-layouts  3.18 us (1%)
    pallas_call x1, Pallas kernels, block(): pl.pallas_call(kernel, name='mlp_line', out_shape=(jax.ShapeDtypeStruct((...  235 us

profile of v1, /device:TPU:0, one launch (start us, length us, event | category | flops | bytes accessed | tf_op | source)
XLA Modules:
  0.0 237.9 jit_solution(7136889138349308486)
XLA Ops:
  0.0 234.8 %mlp_line.1 = (bf16[224,5120]{1,0:T(8,128)(2,1)}, bf16[16,112,5120]{2,1,0:T(8,128)(2,1)}) custom-call(bf16[224,5120]{1,0:T(8,128)(2,1)} %x.1, bf16[5120,1536]{1,0:T(8,128)(2,1)} %wg.1, bf16[5120,1536]{1,0:T(8,128)(2,1)} %wu.1, bf16[1536,5120]{1,0:T(8,128)(2,1)} %wd.1), custom_call_target="tpu_custom_call" | custom-call | tf_op jit(solution)/shard_map/mlp_line/pallas_call | solution.py:302
  234.8 3.2 %copy.6 = bf16[224,5120]{1,0:T(8,128)(2,1)} copy(bf16[224,5120]{1,0:T(8,128)(2,1)} %get-tuple-element.6) | data formatting | bytes 4587520

commit v2 on v1

--- a/solution.py
+++ b/solution.py
@@ -10,7 +10,9 @@
 SUBS = 2
 CHUNKS = 10
 LAG = 3
+HOLD = 2
 RING = 4
+GIVES = 3
 TILES = 3
 
 
@@ -44,6 +46,23 @@
     def cols(i, n):
         return pl.ds(pl.multiple_of(i * n, n), n)
 
+    def give_own(h):
+        spot = xb.at[pl.ds(half, half)] if h == 0 else xg.at[slab(z, h, c)]
+        return remote(x.at[pl.ds(h * half, half)], spot, os.at[h], orr.at[h], other)
+
+    def load(src, i):
+        return pltpu.make_async_copy(src, xb.at[pl.ds(i * half, half)], x_s.at[i])
+
+    def weight(k, src, dst, i):
+        return pltpu.make_async_copy(src.at[:, cols(i, tile)], dst.at[:, cols(i, tile)], w_s.at[k, i])
+
+    load(x.at[pl.ds(0, half)], 0).start()
+    for i in range(TILES):
+        weight(0, wg, wgv, i).start()
+        weight(1, wu, wuv, i).start()
+    load_wd = pltpu.make_async_copy(wd, wdv, w_s.at[2, 0])
+    load_wd.start()
+
     barrier = pltpu.get_barrier_semaphore()
     pl.semaphore_signal(barrier, inc=1, device_id={"tp": other}, device_id_type=MESH)
     for d in range(2):
@@ -58,30 +77,19 @@
             ag_s.at[d, slot, i], ag_r.at[d, slot, i], ahead[d],
         )
 
-    def give_own(h):
-        return remote(x.at[pl.ds(h * half, half)], xg.at[slab(z, h, c)], os.at[h], orr.at[h], other)
-
     for d in range(2):
         @pl.when(pos[d] < CHIPS - 1)
         def _():
             for i in range(SUBS):
                 send_own(d, 0, 0, i).start()
     give_own(0).start()
-
-    def weight(k, src, dst, i):
-        return pltpu.make_async_copy(src.at[:, cols(i, tile)], dst.at[:, cols(i, tile)], w_s.at[k, i])
-
-    for i in range(TILES):
-        weight(0, wg, wgv, i).start()
-        weight(1, wu, wuv, i).start()
-    load_wd = pltpu.make_async_copy(wd, wdv, w_s.at[2, 0])
-    load_wd.start()
     give_own(1).start()
 
     def hidden_slot(a):
-        return jnp.where(a == 0, 0, 1 + (a - 1) % 3)
-
-    def forward(s):
+        return jnp.where(a < 2, a, 2 + (a - 2) % 3)
+
+    def forward(n):
+        s = n - 1
         far = CHIPS - 1 - inner
         j = jnp.where(s <= far, inner + s, inner + 2 * far + 1 - s)
         h = jnp.where(s <= far, 0, 1)
@@ -92,33 +100,36 @@
         j = jnp.where(low, j, CHIPS - 1 - j)
         came = jnp.where(low, 1, 0)
         came = jnp.where(near, 1 - came, came)
-        mine = pltpu.make_async_copy(x.at[pl.ds(0, half)], xb.at[pl.ds(0, half)], x_s.at[0])
-        theirs = pltpu.make_async_copy(xg.at[0], xb.at[pl.ds(half, half)], x_s.at[1])
-
-        @pl.when((s == 0) | (s == 7))
-        def _():
-            ho = s // 7
-            pltpu.make_async_copy(
-                x.at[pl.ds(pl.multiple_of(ho * half, half), half)], xb.at[pl.ds(0, half)], x_s.at[0]
-            ).start()
-            give_own(ho).wait_recv()
-            pltpu.make_async_copy(xg.at[slab(z, ho, 1 - c)], xb.at[pl.ds(half, half)], x_s.at[1]).start()
-
-        @pl.when((s > 0) & (s < 7))
-        def _():
-            pltpu.make_async_copy(xg.at[slab(j, h, c)], xb.at[pl.ds(0, half)], x_s.at[0]).start()
+
+        @pl.when(n == 0)
+        def _():
+            give_own(0).wait_recv()
+
+        @pl.when(n == 1)
+        def _():
+            load(x.at[pl.ds(half, half)], 0).start()
+            give_own(1).wait_recv()
+            load(xg.at[slab(z, 1, 1 - c)], 1).start()
+
+        @pl.when(n > 1)
+        def _():
+            load(xg.at[slab(j, h, c)], 0).start()
             for i in range(SUBS):
                 spot = xg.at[slab(j, h, 1 - c), rows(i)]
                 remote(spot, spot, dd_s.at[came, slot, i], dd_r.at[came, slot, i], other).wait_recv()
-            pltpu.make_async_copy(xg.at[slab(j, h, 1 - c)], xb.at[pl.ds(half, half)], x_s.at[1]).start()
-
-        mine.wait()
-        theirs.wait()
-        hs = hidden_slot(s)
+            load(xg.at[slab(j, h, 1 - c)], 1).start()
+
+        load(xg.at[0], 0).wait()
+
+        @pl.when(n > 0)
+        def _():
+            load(xg.at[0], 1).wait()
+
+        hs = hidden_slot(n)
 
         @pl.loop(0, TILES)
         def _(i):
-            @pl.when(s == 0)
+            @pl.when(n == 0)
             def _():
                 weight(0, wg, wgv, i).wait()
                 weight(1, wu, wuv, i).wait()
@@ -129,7 +140,7 @@
 
     def relay(s, i):
         for d in range(2):
-            @pl.when((pos[d] > 0) & (s < 2 * pos[d]))
+            @pl.when((s >= 0) & (s < 2 * pos[d]))
             def _():
                 p = pos[d] - 1
                 j = jnp.where(s <= p, p - s, s - p - 1)
@@ -144,21 +155,21 @@
                 remote(spot, spot, dd_s.at[d, s, i], dd_r.at[d, s, i], other).start()
 
     def exchange(b, i):
-        return remote(give.at[b, i % RING], take.at[b, i], give_s.at[b, i % RING], take_r.at[b, i], other)
+        return remote(give.at[b, i % GIVES], take.at[b, i], give_s.at[b, i % GIVES], take_r.at[b, i], other)
 
     def make_term(b, hs, i):
         value = jnp.dot(hid[hs], wdv[:, cols(i, width)], preferred_element_type=f32)
         term[b, i % RING] = value[:half]
 
-        @pl.when(i >= RING)
-        def _():
-            exchange(b, i - RING).wait_send()
-
-        give[b, i % RING] = value[half:].astype(bf16)
+        @pl.when(i >= GIVES)
+        def _():
+            exchange(b, i - GIVES).wait_send()
+
+        give[b, i % GIVES] = value[half:].astype(bf16)
         exchange(b, i).start()
 
     def drain(b):
-        for i in range(CHUNKS - RING, CHUNKS):
+        for i in range(CHUNKS - GIVES, CHUNKS):
             exchange(b, i).wait_send()
 
     def to_ring(d, i):
@@ -172,20 +183,19 @@
 
         @pl.when(active[0] | active[1])
         def _():
-            @pl.loop(0, CHUNKS + LAG)
+            @pl.loop(0, CHUNKS + LAG + HOLD)
             def _(i):
                 for d in range(2):
                     far = low if d == 0 else jnp.logical_not(low)
 
                     @pl.when(active[d] & (i < CHUNKS))
                     def _():
-                        make_term(d, hidden_slot(s - jnp.where(far, 2 * inner, 0)), i)
-
-                for d in range(2):
-                    @pl.when(active[d] & (i >= LAG))
+                        make_term(d, hidden_slot(s + 1 - jnp.where(far, 2 * inner, 0)), i)
+
+                for d in range(2):
+                    @pl.when(active[d] & (i >= LAG) & (i < CHUNKS + LAG))
                     def _():
                         k = i - LAG
-                        r = s - 2 * pos[d] - 1
                         exchange(d, k).wait_recv()
 
                         @pl.when(pos[d] > 0)
@@ -194,11 +204,22 @@
                             term[d, k % RING] = term[d, k % RING] + rin[d, k].astype(f32)
                             pl.semaphore_signal(credit.at[d], inc=1, device_id={"tp": behind[d]}, device_id_type=MESH)
 
-                        @pl.when(r >= 1)
+                for d in range(2):
+                    @pl.when(active[d] & (i >= LAG) & (i < CHUNKS + LAG))
+                    def _():
+                        k = i - LAG
+
+                        @pl.when(s - 2 * pos[d] - 1 >= 1)
                         def _():
                             to_ring(d, k).wait_send()
 
                         snd[d, k] = (term[d, k % RING] + take[d, k].astype(f32)).astype(bf16)
+
+                for d in range(2):
+                    @pl.when(active[d] & (i >= LAG + HOLD))
+                    def _():
+                        k = i - LAG - HOLD
+                        r = s - 2 * pos[d] - 1
 
                         @pl.when(r == 0)
                         def _():
@@ -247,16 +268,17 @@
         drain(h)
 
     @pl.loop(0, 8)
-    def _(s):
+    def _(n):
+        s = n - 1
         for d in range(2):
             @pl.when((pos[d] < CHIPS - 1) & (s == 2 * pos[d]))
             def _():
                 for i in range(SUBS):
                     send_own(d, 1, s + 1, i).start()
 
-        forward(s)
-
-        @pl.when(s == 0)
+        forward(n)
+
+        @pl.when(n == 1)
         def _():
             load_wd.wait()
 
@@ -313,12 +335,12 @@
             pltpu.VMEM((depth, hidden), bf16),
             pltpu.VMEM((hidden, depth), bf16),
             pltpu.VMEM((n, depth), bf16),
-            pltpu.VMEM((4, n, hidden), bf16),
+            pltpu.VMEM((5, n, hidden), bf16),
             pltpu.VMEM((2, CHUNKS, half, width), bf16),
             pltpu.VMEM((2, CHUNKS, half, width), bf16),
             pltpu.VMEM((2, CHUNKS, half, width), bf16),
             pltpu.VMEM((2, RING, half, width), f32),
-            pltpu.VMEM((2, RING, half, width), bf16),
+            pltpu.VMEM((2, GIVES, half, width), bf16),
             pltpu.VMEM((2, CHUNKS, half, width), bf16),
             sem.DMA((2, 6, SUBS)),
             sem.DMA((2, 6, SUBS)),
@@ -329,7 +351,7 @@
             sem.DMA((2, CHUNKS)),
             sem.DMA((2, CHUNKS)),
             sem.DMA((2, CHUNKS)),
-            sem.DMA((2, RING)),
+            sem.DMA((2, GIVES)),
             sem.DMA((2, CHUNKS)),
             sem.DMA((2, CHUNKS)),
             sem.DMA((3, TILES)),

time: 238 us -> 209 us (0.88)
  Pallas kernels: 235 us -> 206 us
    pallas_call x1, Pallas kernels: 235 us -> 206 us  [block(): pl.pallas_call(kernel, name='mlp_line', out_shape=(jax.ShapeDtypeStruct((...]
where the time goes in v2:
time: 209 us
  Pallas kernels  206 us (99%)
  local copies, waits for them, and re-layouts  3.18 us (2%)
    pallas_call x1, Pallas kernels, block(): pl.pallas_call(kernel, name='mlp_line', out_shape=(jax.ShapeDtypeStruct((...  206 us

profile of v2, /device:TPU:0, one launch (start us, length us, event | category | flops | bytes accessed | tf_op | source)
XLA Modules:
  0.0 209.1 jit_solution(5229637962900410252)
XLA Ops:
  0.0 205.9 %mlp_line.1 = (bf16[224,5120]{1,0:T(8,128)(2,1)}, bf16[16,112,5120]{2,1,0:T(8,128)(2,1)}) custom-call(bf16[224,5120]{1,0:T(8,128)(2,1)} %x.1, bf16[5120,1536]{1,0:T(8,128)(2,1)} %wg.1, bf16[5120,1536]{1,0:T(8,128)(2,1)} %wu.1, bf16[1536,5120]{1,0:T(8,128)(2,1)} %wd.1), custom_call_target="tpu_custom_call" | custom-call | tf_op jit(solution)/shard_map/mlp_line/pallas_call | solution.py:324
  205.9 3.2 %copy.6 = bf16[224,5120]{1,0:T(8,128)(2,1)} copy(bf16[224,5120]{1,0:T(8,128)(2,1)} %get-tuple-element.6) | data formatting | bytes 4587520

commit v3 on v2

--- a/solution.py
+++ b/solution.py
@@ -17,9 +17,9 @@
 
 
 def kernel(
-    x, wg, wu, wd, y, xg,
-    wgv, wuv, wdv, xb, hid, rin, own0, snd, term, give, take,
-    ag_s, ag_r, dd_s, dd_r, os, orr, rin_r, own_r, snd_s, give_s, take_r, y_s, w_s, x_s, credit,
+    x, wg, wu, wd, xb, xg,
+    wgv, wuv, wdv, hid, rin, own0, snd, term, give, take,
+    ag_s, ag_r, dd_s, dd_r, os, orr, rin_r, own_r, snd_s, give_s, take_r, w_s, x_s, credit,
 ):
     f32, bf16 = jnp.float32, jnp.bfloat16
     half, depth = x.shape[0] // 2, x.shape[1]
@@ -238,10 +238,6 @@
                 def _():
                     drain(d)
 
-    def write(h, i):
-        spot = (pl.ds(h * half, half), cols(i, width))
-        return pltpu.make_async_copy(xb.at[spot], y.at[spot], y_s.at[h, i])
-
     def finish(h, hs):
         came, sems = (own0, own_r) if h == 0 else (rin, rin_r)
 
@@ -263,7 +259,6 @@
                         term[h, k % RING] = term[h, k % RING] + came[d, k].astype(f32)
 
                 xb[pl.ds(h * half, half), cols(k, width)] = term[h, k % RING].astype(bf16)
-                write(h, k).start()
 
         drain(h)
 
@@ -287,18 +282,11 @@
         for i in range(1, SUBS):
             relay(s, i)
 
-    finish(0, 0)
-    finish(1, 1)
-
     for h in range(2):
         give_own(h).wait_send()
-
-        @pl.loop(0, CHUNKS)
-        def _(i):
-            write(h, i).wait()
-
     for d in range(2):
-        for s in range(6):
+        @pl.loop(0, 6)
+        def _(s):
             for i in range(SUBS):
                 spot = xg.at[0, rows(i)]
 
@@ -310,6 +298,9 @@
                 def _():
                     remote(spot, spot, dd_s.at[d, s, i], dd_r.at[d, s, i], other).wait_send()
 
+    finish(0, 0)
+    finish(1, 1)
+    for d in range(2):
         @pl.when(pos[d] < CHIPS - 1)
         def _():
             @pl.loop(0, CHUNKS)
@@ -325,16 +316,15 @@
         kernel,
         name="mlp_line",
         out_shape=(
-            jax.ShapeDtypeStruct((n, depth), bf16),
+            pltpu.VMEM((n, depth), bf16),
             jax.ShapeDtypeStruct((4 * CHIPS, half, depth), bf16),
         ),
         in_specs=[pl.BlockSpec(memory_space=pl.ANY)] * 4,
-        out_specs=(pl.BlockSpec(memory_space=pl.ANY),) * 2,
+        out_specs=(pl.BlockSpec(memory_space=pltpu.VMEM), pl.BlockSpec(memory_space=pl.ANY)),
         scratch_shapes=[
             pltpu.VMEM((depth, hidden), bf16),
             pltpu.VMEM((depth, hidden), bf16),
             pltpu.VMEM((hidden, depth), bf16),
-            pltpu.VMEM((n, depth), bf16),
             pltpu.VMEM((5, n, hidden), bf16),
             pltpu.VMEM((2, CHUNKS, half, width), bf16),
             pltpu.VMEM((2, CHUNKS, half, width), bf16),
@@ -353,13 +343,12 @@
             sem.DMA((2, CHUNKS)),
             sem.DMA((2, GIVES)),
             sem.DMA((2, CHUNKS)),
-            sem.DMA((2, CHUNKS)),
             sem.DMA((3, TILES)),
             sem.DMA((2,)),
             sem.REGULAR((2,)),
         ],
         compiler_params=pltpu.CompilerParams(
-            collective_id=0, has_side_effects=True, vmem_limit_bytes=67_043_328
+            collective_id=0, has_side_effects=True, vmem_limit_bytes=64_700_000
         ),
     )(x, w_gate, w_up, w_down)[0]
 

time: 209 us -> 205 us (0.981)
    pallas_call x1, Pallas kernels: 206 us -> 204 us  [block(): pl.pallas_call(kernel, name='mlp_line', out_shape=(pltpu.VMEM((n, depth),...]
where the time goes in v3:
time: 205 us
  Pallas kernels  204 us (100%)
    pallas_call x1, Pallas kernels, block(): pl.pallas_call(kernel, name='mlp_line', out_shape=(pltpu.VMEM((n, depth),...  204 us

profile of v3, /device:TPU:0, one launch (start us, length us, event | category | flops | bytes accessed | tf_op | source)
XLA Modules:
  0.0 205.1 jit_solution(15549011571373041670)
XLA Ops:
  0.0 203.7 %mlp_line.1 = (bf16[224,5120]{1,0:T(8,128)(2,1)S(1)}, bf16[16,112,5120]{2,1,0:T(8,128)(2,1)}) custom-call(bf16[224,5120]{1,0:T(8,128)(2,1)} %x.1, bf16[5120,1536]{1,0:T(8,128)(2,1)} %wg.1, bf16[5120,1536]{1,0:T(8,128)(2,1)} %wu.1, bf16[1536,5120]{1,0:T(8,128)(2,1)} %wd.1), custom_call_target="tpu_custom_call" | custom-call | tf_op jit(solution)/shard_map/mlp_line/pallas_call | solution.py:315
  203.7 1.4 copy.6

commit v4 on v3

--- a/solution.py
+++ b/solution.py
@@ -48,33 +48,33 @@
 
     def give_own(h):
         spot = xb.at[pl.ds(half, half)] if h == 0 else xg.at[slab(z, h, c)]
-        return remote(x.at[pl.ds(h * half, half)], spot, os.at[h], orr.at[h], other)
+        return remote(x.at[pl.ds(h * half, half)], spot, os, orr.at[h], other)
 
     def load(src, i):
         return pltpu.make_async_copy(src, xb.at[pl.ds(i * half, half)], x_s.at[i])
 
     def weight(k, src, dst, i):
-        return pltpu.make_async_copy(src.at[:, cols(i, tile)], dst.at[:, cols(i, tile)], w_s.at[k, i])
+        return pltpu.make_async_copy(src.at[:, cols(i, tile)], dst.at[:, cols(i, tile)], w_s.at[k * TILES + i])
+
+    barrier = pltpu.get_barrier_semaphore()
+    pl.semaphore_signal(barrier, inc=1, device_id={"tp": other}, device_id_type=MESH)
+    for d in range(2):
+        @pl.when(pos[d] < CHIPS - 1)
+        def _():
+            pl.semaphore_signal(barrier, inc=1, device_id={"tp": ahead[d]}, device_id_type=MESH)
 
     load(x.at[pl.ds(0, half)], 0).start()
     for i in range(TILES):
         weight(0, wg, wgv, i).start()
         weight(1, wu, wuv, i).start()
-    load_wd = pltpu.make_async_copy(wd, wdv, w_s.at[2, 0])
+    load_wd = pltpu.make_async_copy(wd, wdv, w_s.at[2 * TILES])
     load_wd.start()
-
-    barrier = pltpu.get_barrier_semaphore()
-    pl.semaphore_signal(barrier, inc=1, device_id={"tp": other}, device_id_type=MESH)
-    for d in range(2):
-        @pl.when(pos[d] < CHIPS - 1)
-        def _():
-            pl.semaphore_signal(barrier, inc=1, device_id={"tp": ahead[d]}, device_id_type=MESH)
     pl.semaphore_wait(barrier, 1 + jnp.minimum(z, 1) + jnp.minimum(CHIPS - 1 - z, 1))
 
     def send_own(d, h, slot, i):
         return remote(
             x.at[pl.ds(h * half + i * piece, piece)], xg.at[slab(z, h, c), rows(i)],
-            ag_s.at[d, slot, i], ag_r.at[d, slot, i], ahead[d],
+            ag_s.at[d], ag_r.at[d, slot, i], ahead[d],
         )
 
     for d in range(2):
@@ -114,10 +114,9 @@
         @pl.when(n > 1)
         def _():
             load(xg.at[slab(j, h, c)], 0).start()
-            for i in range(SUBS):
-                spot = xg.at[slab(j, h, 1 - c), rows(i)]
-                remote(spot, spot, dd_s.at[came, slot, i], dd_r.at[came, slot, i], other).wait_recv()
-            load(xg.at[slab(j, h, 1 - c)], 1).start()
+            spot = xg.at[slab(j, h, 1 - c)]
+            remote(spot, spot, dd_s.at[came], dd_r.at[came, slot], other).wait_recv()
+            load(spot, 1).start()
 
         load(xg.at[0], 0).wait()
 
@@ -146,13 +145,13 @@
                 j = jnp.where(s <= p, p - s, s - p - 1)
                 h = jnp.where(s <= p, 0, 1)
                 spot = xg.at[slab(j if d == 0 else CHIPS - 1 - j, h, c), rows(i)]
-                remote(spot, spot, ag_s.at[d, s, i], ag_r.at[d, s, i], ahead[d]).wait_recv()
+                remote(spot, spot, ag_s.at[d], ag_r.at[d, s, i], ahead[d]).wait_recv()
 
                 @pl.when(pos[d] < CHIPS - 1)
                 def _():
-                    remote(spot, spot, ag_s.at[d, s + 1, i], ag_r.at[d, s + 1, i], ahead[d]).start()
-
-                remote(spot, spot, dd_s.at[d, s, i], dd_r.at[d, s, i], other).start()
+                    remote(spot, spot, ag_s.at[d], ag_r.at[d, s + 1, i], ahead[d]).start()
+
+                remote(spot, spot, dd_s.at[d], dd_r.at[d, s], other).start()
 
     def exchange(b, i):
         return remote(give.at[b, i % GIVES], take.at[b, i], give_s.at[b, i % GIVES], take_r.at[b, i], other)
@@ -176,7 +175,7 @@
         return remote(snd.at[d, i], rin.at[d, i], snd_s.at[d, i], rin_r.at[d, i], ahead[d])
 
     def to_own(d, i):
-        return remote(snd.at[d, i], own0.at[d, i], snd_s.at[d, i], own_r.at[d, i], ahead[d])
+        return remote(snd.at[d, i], own0.at[d, i], snd_s.at[d, i], own_r.at[d], ahead[d])
 
     def scatter(s):
         active = [(pos[d] < CHIPS - 1) & (s >= 2 * pos[d] + 1) & (s < 7) for d in range(2)]
@@ -239,7 +238,12 @@
                     drain(d)
 
     def finish(h, hs):
-        came, sems = (own0, own_r) if h == 0 else (rin, rin_r)
+        came = own0 if h == 0 else rin
+        if h == 0:
+            for d in range(2):
+                @pl.when(pos[d] > 0)
+                def _():
+                    remote(own0.at[d], own0.at[d], snd_s.at[d, 0], own_r.at[d], ahead[d]).wait_recv()
 
         @pl.loop(0, CHUNKS + LAG)
         def _(i):
@@ -255,7 +259,8 @@
                 for d in range(2):
                     @pl.when(pos[d] > 0)
                     def _():
-                        remote(came.at[d, k], came.at[d, k], snd_s.at[d, k], sems.at[d, k], ahead[d]).wait_recv()
+                        if h == 1:
+                            to_ring(d, k).wait_recv()
                         term[h, k % RING] = term[h, k % RING] + came[d, k].astype(f32)
 
                 xb[pl.ds(h * half, half), cols(k, width)] = term[h, k % RING].astype(bf16)
@@ -271,32 +276,35 @@
                 for i in range(SUBS):
                     send_own(d, 1, s + 1, i).start()
 
+        @pl.when(n == 1)
+        def _():
+            relay(0, 0)
+
         forward(n)
 
         @pl.when(n == 1)
         def _():
             load_wd.wait()
 
-        relay(s, 0)
+        @pl.when(n > 1)
+        def _():
+            relay(s, 0)
+
         scatter(s)
         for i in range(1, SUBS):
             relay(s, i)
 
-    for h in range(2):
-        give_own(h).wait_send()
+    pltpu.make_async_copy(x, x, os).wait()
     for d in range(2):
-        @pl.loop(0, 6)
-        def _(s):
-            for i in range(SUBS):
-                spot = xg.at[0, rows(i)]
-
-                @pl.when((pos[d] < CHIPS - 1) & (s < 2 * pos[d] + 2))
-                def _():
-                    remote(spot, spot, ag_s.at[d, s, i], ag_r.at[d, s, i], ahead[d]).wait_send()
-
-                @pl.when(s < 2 * pos[d])
-                def _():
-                    remote(spot, spot, dd_s.at[d, s, i], dd_r.at[d, s, i], other).wait_send()
+        for p in range(CHIPS):
+            @pl.when(pos[d] == p)
+            def _():
+                if p < CHIPS - 1:
+                    spot = xg.at[pl.ds(0, 2 * p + 2)]
+                    remote(spot, spot, ag_s.at[d], ag_r.at[d, 0, 0], ahead[d]).wait_send()
+                if p > 0:
+                    spot = xg.at[pl.ds(0, 2 * p)]
+                    remote(spot, spot, dd_s.at[d], dd_r.at[d, 0], other).wait_send()
 
     finish(0, 0)
     finish(1, 1)
@@ -332,18 +340,18 @@
             pltpu.VMEM((2, RING, half, width), f32),
             pltpu.VMEM((2, GIVES, half, width), bf16),
             pltpu.VMEM((2, CHUNKS, half, width), bf16),
+            sem.DMA((2,)),
             sem.DMA((2, 6, SUBS)),
-            sem.DMA((2, 6, SUBS)),
-            sem.DMA((2, 6, SUBS)),
-            sem.DMA((2, 6, SUBS)),
-            sem.DMA((2,)),
+            sem.DMA((2,)),
+            sem.DMA((2, 6)),
+            sem.DMA,
             sem.DMA((2,)),
             sem.DMA((2, CHUNKS)),
-            sem.DMA((2, CHUNKS)),
+            sem.DMA((2,)),
             sem.DMA((2, CHUNKS)),
             sem.DMA((2, GIVES)),
             sem.DMA((2, CHUNKS)),
-            sem.DMA((3, TILES)),
+            sem.DMA((2 * TILES + 1,)),
             sem.DMA((2,)),
             sem.REGULAR((2,)),
         ],

time: 205 us -> 205 us (level)
  no operation moved by 1% of the time
where the time goes in v4:
time: 205 us; the launch traced here: 204 us
  Pallas kernels  203 us (99%)
    pallas_call x1, Pallas kernels, block(): pl.pallas_call(kernel, name='mlp_line', out_shape=(pltpu.VMEM((n, depth),...  203 us

profile of v4, /device:TPU:0, one launch (start us, length us, event | category | flops | bytes accessed | tf_op | source)
XLA Modules:
  0.0 204.3 jit_solution(17667424863522858493)
XLA Ops:
  0.0 202.9 %mlp_line.1 = (bf16[224,5120]{1,0:T(8,128)(2,1)S(1)}, bf16[16,112,5120]{2,1,0:T(8,128)(2,1)}) custom-call(bf16[224,5120]{1,0:T(8,128)(2,1)} %x.1, bf16[5120,1536]{1,0:T(8,128)(2,1)} %wg.1, bf16[5120,1536]{1,0:T(8,128)(2,1)} %wu.1, bf16[1536,5120]{1,0:T(8,128)(2,1)} %wd.1), custom_call_target="tpu_custom_call" | custom-call | tf_op jit(solution)/shard_map/mlp_line/pallas_call | solution.py:323
  202.9 1.4 copy.6

commit v5 on v4

--- a/solution.py
+++ b/solution.py
@@ -19,7 +19,7 @@
 def kernel(
     x, wg, wu, wd, xb, xg,
     wgv, wuv, wdv, hid, rin, own0, snd, term, give, take,
-    ag_s, ag_r, dd_s, dd_r, os, orr, rin_r, own_r, snd_s, give_s, take_r, w_s, x_s, credit,
+    ag_s, ag_r, dd_s, dd_r, os, orr, rin_r, own_r, snd_s, give_s, take_r, w_s, x_s, credit, hello,
 ):
     f32, bf16 = jnp.float32, jnp.bfloat16
     half, depth = x.shape[0] // 2, x.shape[1]
@@ -40,6 +40,9 @@
     def slab(j, h, core):
         return (j * 2 + h) * 2 + core
 
+    def place(d, slot):
+        return slot if d == 0 else 2 * CHIPS - 3 - slot
+
     def rows(i):
         return pl.ds(i * piece, piece)
 
@@ -57,33 +60,41 @@
         return pltpu.make_async_copy(src.at[:, cols(i, tile)], dst.at[:, cols(i, tile)], w_s.at[k * TILES + i])
 
     barrier = pltpu.get_barrier_semaphore()
+
+    @pl.when(z < CHIPS - 1)
+    def _():
+        pl.semaphore_signal(barrier, inc=1, device_id={"tp": ahead[0]}, device_id_type=MESH)
+
     pl.semaphore_signal(barrier, inc=1, device_id={"tp": other}, device_id_type=MESH)
-    for d in range(2):
-        @pl.when(pos[d] < CHIPS - 1)
-        def _():
-            pl.semaphore_signal(barrier, inc=1, device_id={"tp": ahead[d]}, device_id_type=MESH)
-
     load(x.at[pl.ds(0, half)], 0).start()
     for i in range(TILES):
         weight(0, wg, wgv, i).start()
         weight(1, wu, wuv, i).start()
     load_wd = pltpu.make_async_copy(wd, wdv, w_s.at[2 * TILES])
     load_wd.start()
-    pl.semaphore_wait(barrier, 1 + jnp.minimum(z, 1) + jnp.minimum(CHIPS - 1 - z, 1))
-
     def send_own(d, h, slot, i):
         return remote(
             x.at[pl.ds(h * half + i * piece, piece)], xg.at[slab(z, h, c), rows(i)],
-            ag_s.at[d], ag_r.at[d, slot, i], ahead[d],
+            ag_s.at[d], ag_r.at[place(d, slot), i], ahead[d],
         )
 
-    for d in range(2):
-        @pl.when(pos[d] < CHIPS - 1)
-        def _():
-            for i in range(SUBS):
-                send_own(d, 0, 0, i).start()
+    pl.semaphore_wait(barrier, 1 + jnp.minimum(z, 1))
+
+    @pl.when(z > 0)
+    def _():
+        pl.semaphore_signal(hello, inc=1, device_id={"tp": ahead[1]}, device_id_type=MESH)
+        for i in range(SUBS):
+            send_own(1, 0, 0, i).start()
+
     give_own(0).start()
     give_own(1).start()
+
+    @pl.when(z < CHIPS - 1)
+    def _():
+        pl.semaphore_wait(hello, 1)
+        for i in range(SUBS):
+            send_own(0, 0, 0, i).start()
+
 
     def hidden_slot(a):
         return jnp.where(a < 2, a, 2 + (a - 2) % 3)
@@ -115,7 +126,7 @@
         def _():
             load(xg.at[slab(j, h, c)], 0).start()
             spot = xg.at[slab(j, h, 1 - c)]
-            remote(spot, spot, dd_s.at[came], dd_r.at[came, slot], other).wait_recv()
+            remote(spot, spot, dd_s.at[came], dd_r.at[jnp.where(came == 0, slot, 2 * CHIPS - 3 - slot)], other).wait_recv()
             load(spot, 1).start()
 
         load(xg.at[0], 0).wait()
@@ -145,13 +156,13 @@
                 j = jnp.where(s <= p, p - s, s - p - 1)
                 h = jnp.where(s <= p, 0, 1)
                 spot = xg.at[slab(j if d == 0 else CHIPS - 1 - j, h, c), rows(i)]
-                remote(spot, spot, ag_s.at[d], ag_r.at[d, s, i], ahead[d]).wait_recv()
+                remote(spot, spot, ag_s.at[d], ag_r.at[place(d, s), i], ahead[d]).wait_recv()
 
                 @pl.when(pos[d] < CHIPS - 1)
                 def _():
-                    remote(spot, spot, ag_s.at[d], ag_r.at[d, s + 1, i], ahead[d]).start()
-
-                remote(spot, spot, dd_s.at[d], dd_r.at[d, s], other).start()
+                    remote(spot, spot, ag_s.at[d], ag_r.at[place(d, s + 1), i], ahead[d]).start()
+
+                remote(spot, spot, dd_s.at[d], dd_r.at[place(d, s)], other).start()
 
     def exchange(b, i):
         return remote(give.at[b, i % GIVES], take.at[b, i], give_s.at[b, i % GIVES], take_r.at[b, i], other)
@@ -301,10 +312,10 @@
             def _():
                 if p < CHIPS - 1:
                     spot = xg.at[pl.ds(0, 2 * p + 2)]
-                    remote(spot, spot, ag_s.at[d], ag_r.at[d, 0, 0], ahead[d]).wait_send()
+                    remote(spot, spot, ag_s.at[d], ag_r.at[0, 0], ahead[d]).wait_send()
                 if p > 0:
                     spot = xg.at[pl.ds(0, 2 * p)]
-                    remote(spot, spot, dd_s.at[d], dd_r.at[d, 0], other).wait_send()
+                    remote(spot, spot, dd_s.at[d], dd_r.at[0], other).wait_send()
 
     finish(0, 0)
     finish(1, 1)
@@ -341,9 +352,9 @@
             pltpu.VMEM((2, GIVES, half, width), bf16),
             pltpu.VMEM((2, CHUNKS, half, width), bf16),
             sem.DMA((2,)),
-            sem.DMA((2, 6, SUBS)),
-            sem.DMA((2,)),
-            sem.DMA((2, 6)),
+            sem.DMA((6, SUBS)),
+            sem.DMA((2,)),
+            sem.DMA((6,)),
             sem.DMA,
             sem.DMA((2,)),
             sem.DMA((2, CHUNKS)),
@@ -354,6 +365,7 @@
             sem.DMA((2 * TILES + 1,)),
             sem.DMA((2,)),
             sem.REGULAR((2,)),
+            sem.REGULAR,
         ],
         compiler_params=pltpu.CompilerParams(
             collective_id=0, has_side_effects=True, vmem_limit_bytes=64_700_000

time: 205 us -> 204 us (level)
  no operation moved by 1% of the time
where the time goes in v5:
time: 204 us
  Pallas kernels  202 us (99%)
    pallas_call x1, Pallas kernels, block(): pl.pallas_call(kernel, name='mlp_line', out_shape=(pltpu.VMEM((n, depth),...  202 us

profile of v5, /device:TPU:0, one launch (start us, length us, event | category | flops | bytes accessed | tf_op | source)
XLA Modules:
  0.0 203.5 jit_solution(16081489738812257483)
XLA Ops:
  0.0 202.1 %mlp_line.1 = (bf16[224,5120]{1,0:T(8,128)(2,1)S(1)}, bf16[16,112,5120]{2,1,0:T(8,128)(2,1)}) custom-call(bf16[224,5120]{1,0:T(8,128)(2,1)} %x.1, bf16[5120,1536]{1,0:T(8,128)(2,1)} %wg.1, bf16[5120,1536]{1,0:T(8,128)(2,1)} %wu.1, bf16[1536,5120]{1,0:T(8,128)(2,1)} %wd.1), custom_call_target="tpu_custom_call" | custom-call | tf_op jit(solution)/shard_map/mlp_line/pallas_call | solution.py:334
  202.1 1.4 copy.6

commit v6 on v5

--- a/solution.py
+++ b/solution.py
@@ -8,11 +8,11 @@
 MESH = pl.DeviceIdType.MESH
 CHIPS = 4
 SUBS = 2
-CHUNKS = 10
-LAG = 3
-HOLD = 2
-RING = 4
-GIVES = 3
+CHUNKS = 5
+LAG = 1
+HOLD = 1
+RING = 2
+GIVES = 1
 TILES = 3
 
 
@@ -83,6 +83,11 @@
     @pl.when(z > 0)
     def _():
         pl.semaphore_signal(hello, inc=1, device_id={"tp": ahead[1]}, device_id_type=MESH)
+
+    late = (c == 1) & (z == 1)
+
+    @pl.when((z > 0) & jnp.logical_not(late))
+    def _():
         for i in range(SUBS):
             send_own(1, 0, 0, i).start()
 
@@ -94,6 +99,11 @@
         pl.semaphore_wait(hello, 1)
         for i in range(SUBS):
             send_own(0, 0, 0, i).start()
+
+    @pl.when(late)
+    def _():
+        for i in range(SUBS):
+            send_own(1, 0, 0, i).start()
 
 
     def hidden_slot(a):
@@ -168,14 +178,15 @@
         return remote(give.at[b, i % GIVES], take.at[b, i], give_s.at[b, i % GIVES], take_r.at[b, i], other)
 
     def make_term(b, hs, i):
-        value = jnp.dot(hid[hs], wdv[:, cols(i, width)], preferred_element_type=f32)
-        term[b, i % RING] = value[:half]
-
         @pl.when(i >= GIVES)
         def _():
             exchange(b, i - GIVES).wait_send()
 
-        give[b, i % GIVES] = value[half:].astype(bf16)
+        for part in range(2):
+            value = jnp.dot(hid[hs], wdv[:, cols(2 * i + part, width // 2)], preferred_element_type=f32)
+            spot = pl.ds(part * width // 2, width // 2)
+            term[b, i % RING, :, spot] = value[:half]
+            give[b, i % GIVES, :, spot] = value[half:].astype(bf16)
         exchange(b, i).start()
 
     def drain(b):

time: 204 us -> 203 us (level)
  no operation moved by 1% of the time
where the time goes in v6:
time: 203 us; the launch traced here: 202 us
  Pallas kernels  201 us (99%)
    pallas_call x1, Pallas kernels, block(): pl.pallas_call(kernel, name='mlp_line', out_shape=(pltpu.VMEM((n, depth),...  201 us

profile of v6, /device:TPU:0, one launch (start us, length us, event | category | flops | bytes accessed | tf_op | source)
XLA Modules:
  0.0 202.3 jit_solution(3282766815782407660)
XLA Ops:
  0.0 200.9 %mlp_line.1 = (bf16[224,5120]{1,0:T(8,128)(2,1)S(1)}, bf16[16,112,5120]{2,1,0:T(8,128)(2,1)}) custom-call(bf16[224,5120]{1,0:T(8,128)(2,1)} %x.1, bf16[5120,1536]{1,0:T(8,128)(2,1)} %wg.1, bf16[5120,1536]{1,0:T(8,128)(2,1)} %wu.1, bf16[1536,5120]{1,0:T(8,128)(2,1)} %wd.1), custom_call_target="tpu_custom_call" | custom-call | tf_op jit(solution)/shard_map/mlp_line/pallas_call | solution.py:345
  200.9 1.4 copy.6

commit v7 on v6

--- a/solution.py
+++ b/solution.py
@@ -19,7 +19,7 @@
 def kernel(
     x, wg, wu, wd, xb, xg,
     wgv, wuv, wdv, hid, rin, own0, snd, term, give, take,
-    ag_s, ag_r, dd_s, dd_r, os, orr, rin_r, own_r, snd_s, give_s, take_r, w_s, x_s, credit, hello,
+    ag_s, ag_r, dd_s, dd_r, os, orr, rin_r, own_r, snd_s, give_s, take_r, w_s, x_s, credit, hello, beside,
 ):
     f32, bf16 = jnp.float32, jnp.bfloat16
     half, depth = x.shape[0] // 2, x.shape[1]
@@ -65,7 +65,10 @@
     def _():
         pl.semaphore_signal(barrier, inc=1, device_id={"tp": ahead[0]}, device_id_type=MESH)
 
-    pl.semaphore_signal(barrier, inc=1, device_id={"tp": other}, device_id_type=MESH)
+    @pl.when(c == 1)
+    def _():
+        pl.semaphore_signal(barrier, inc=1, device_id={"tp": other}, device_id_type=MESH)
+
     load(x.at[pl.ds(0, half)], 0).start()
     for i in range(TILES):
         weight(0, wg, wgv, i).start()
@@ -78,18 +81,41 @@
             ag_s.at[d], ag_r.at[place(d, slot), i], ahead[d],
         )
 
-    pl.semaphore_wait(barrier, 1 + jnp.minimum(z, 1))
+    @pl.when((c == 0) | (z > 0))
+    def _():
+        pl.semaphore_wait(barrier, 1 - c + jnp.minimum(z, 1))
+
 
     @pl.when(z > 0)
     def _():
         pl.semaphore_signal(hello, inc=1, device_id={"tp": ahead[1]}, device_id_type=MESH)
 
     late = (c == 1) & (z == 1)
+
+    def first(start, count):
+        return remote(
+            x.at[pl.ds(start, count)], xg.at[slab(z, 0, c), pl.ds(start, count)],
+            ag_s.at[1], ag_r.at[place(1, 0), 0], ahead[1],
+        )
 
     @pl.when((z > 0) & jnp.logical_not(late))
     def _():
         for i in range(SUBS):
             send_own(1, 0, 0, i).start()
+
+    head = piece // 4 // 8 * 8
+
+    @pl.when(late)
+    def _():
+        first(0, head).start()
+
+    @pl.when(c == 0)
+    def _():
+        pl.semaphore_signal(beside, inc=1, device_id={"tp": other}, device_id_type=MESH)
+
+    @pl.when(c == 1)
+    def _():
+        pl.semaphore_wait(beside, 1)
 
     give_own(0).start()
     give_own(1).start()
@@ -99,11 +125,6 @@
         pl.semaphore_wait(hello, 1)
         for i in range(SUBS):
             send_own(0, 0, 0, i).start()
-
-    @pl.when(late)
-    def _():
-        for i in range(SUBS):
-            send_own(1, 0, 0, i).start()
 
 
     def hidden_slot(a):
@@ -153,6 +174,12 @@
             def _():
                 weight(0, wg, wgv, i).wait()
                 weight(1, wu, wuv, i).wait()
+
+                @pl.when(late & (i == 0))
+                def _():
+                    first(head, piece - head).start()
+                    for k in range(1, SUBS):
+                        send_own(1, 0, 0, k).start()
 
             gate = jnp.dot(xb[...], wgv[:, cols(i, tile)], preferred_element_type=f32)
             up = jnp.dot(xb[...], wuv[:, cols(i, tile)], preferred_element_type=f32)
@@ -377,6 +404,7 @@
             sem.DMA((2,)),
             sem.REGULAR((2,)),
             sem.REGULAR,
+            sem.REGULAR,
         ],
         compiler_params=pltpu.CompilerParams(
             collective_id=0, has_side_effects=True, vmem_limit_bytes=64_700_000

time: 203 us -> 202 us (level)
  no operation moved by 1% of the time
where the time goes in v7:
time: 202 us
  Pallas kernels  200 us (99%)
    pallas_call x1, Pallas kernels, block(): pl.pallas_call(kernel, name='mlp_line', out_shape=(pltpu.VMEM((n, depth),...  200 us

profile of v7, /device:TPU:0, one launch (start us, length us, event | category | flops | bytes accessed | tf_op | source)
XLA Modules:
  0.0 201.7 jit_solution(15956867670954326279)
XLA Ops:
  0.0 200.3 %mlp_line.1 = (bf16[224,5120]{1,0:T(8,128)(2,1)S(1)}, bf16[16,112,5120]{2,1,0:T(8,128)(2,1)}) custom-call(bf16[224,5120]{1,0:T(8,128)(2,1)} %x.1, bf16[5120,1536]{1,0:T(8,128)(2,1)} %wg.1, bf16[5120,1536]{1,0:T(8,128)(2,1)} %wu.1, bf16[1536,5120]{1,0:T(8,128)(2,1)} %wd.1), custom_call_target="tpu_custom_call" | custom-call | tf_op jit(solution)/shard_map/mlp_line/pallas_call | solution.py:372
  200.3 1.4 copy.6
